TPU v7x, 32 devices: a whole 2x2x4 slice. The times are simulated.
32 devices in a mesh: expert: 4 (over x, core), ffn: 8 (over z, y).
Axes of the slice: x: 2, y: 2, z: 4, core: 2. Of those that a mesh axis runs over, the one named last changes fastest.
Arguments:
- tokens: bfloat16 [4, 32, 4096], P('expert', 'ffn'), may hold values from -6 to 6
- routes: int32 [4, 32, 2], P('expert'), may hold values from 0 to 3, all different within a row; in each aligned block of 32 rows (0 to 31, 32 to 63, ..., all dimensions but the last counted through in order) at most 24 rows name the same one
- router: bfloat16 [4096, 4], replicated, may hold values from -0.09375 to 0.09375
- w_gate: bfloat16 [4, 4096, 12288], P('expert', None, 'ffn'), may hold values from -0.09375 to 0.09375
- w_up: bfloat16 [4, 4096, 12288], P('expert', None, 'ffn'), may hold values from -0.09375 to 0.09375
- w_down: bfloat16 [4, 12288, 4096], P('expert', 'ffn'), may hold values from -0.078125 to 0.078125
- adapter: bfloat16 [4, 4096, 4096], P('expert', None, 'ffn'), may hold values from -0.09375 to 0.09375
- upstream: bfloat16 [4, 32, 4096], P('expert', None, 'ffn'), may hold values from -24 to 24
- bound: float32 [4], P('expert'), may hold values from 2048 to 16384
Outputs:
- adapted: bfloat16 [4, 32, 4096], P('expert', None, 'ffn')
- clipped: bfloat16 [4, 4096, 4096], P('expert', None, 'ffn')
Inputs may be any that keep to these rules, and one draw needn't show every extreme that they name: `routes`: each token names two different experts; for each client at most 24 of its tokens name any one expert, and in some clients some expert is named by exactly 24 tokens.
All inputs are finite; a program needn't handle non-finite values.
Results may differ from a plain program's by a relative error of at most 0.015.
Values may be sent and summed in bfloat16 or wider, within the bound.
A program may use at most 128 MiB of HBM per device.

v0:
```python
import jax
import jax.numpy as jnp
from jax import lax
from jax.sharding import PartitionSpec as P


def slot_table(routed, expert_count):
    named_hits = jnp.sum(
        (routed[:, :, None] == jnp.arange(expert_count, dtype=jnp.int32)[None, None, :]).astype(
            jnp.int32
        ),
        axis=1,
    )
    before = jnp.cumsum(named_hits, axis=0) - named_hits
    return jnp.take_along_axis(before, routed, axis=1)


def pack_rows(token_rows, routed, expert_count, capacity):
    token_count = token_rows.shape[0]
    slot_flat = routed * capacity + slot_table(routed, expert_count)
    owners = jnp.repeat(jnp.arange(token_count, dtype=jnp.int32), 2)
    source = (
        jnp.full((expert_count * capacity,), token_count, jnp.int32)
        .at[slot_flat.reshape(-1)]
        .set(owners)
    )
    padded = jnp.concatenate(
        [token_rows, jnp.zeros((1, token_rows.shape[1]), token_rows.dtype)], axis=0
    )
    return (padded[source].reshape(expert_count, capacity, token_rows.shape[1]), slot_flat)


def mix_weights(token_rows, routed, router):
    logits = jnp.dot(token_rows, router, preferred_element_type=jnp.float32)
    picked = jnp.take_along_axis(logits, routed, axis=1)
    weight_first = jax.nn.sigmoid(picked[:, 0] - picked[:, 1])
    return (weight_first, 1.0 - weight_first)


def per_device(tokens, routes, router, w_gate, w_up, w_down, adapter, upstream, bound):
    expert_count = lax.axis_size("expert")
    gathered = lax.all_gather(tokens, "ffn", axis=1, tiled=True)
    token_rows = gathered[0]
    token_count = token_rows.shape[0]
    model_width = token_rows.shape[1]
    capacity = 3 * token_count // expert_count
    routed = routes[0]
    outgoing, slot_flat = pack_rows(token_rows, routed, expert_count, capacity)
    col_count = adapter.shape[2]
    column = lax.axis_index("ffn") * col_count
    weight_first, weight_second = mix_weights(token_rows, routed, router)
    arrived = lax.all_to_all(outgoing, "expert", split_axis=0, concat_axis=0, tiled=True)
    flat_rows = arrived.reshape(-1, model_width)
    gate_out = jnp.dot(flat_rows, w_gate[0], preferred_element_type=jnp.float32)
    up_out = jnp.dot(flat_rows, w_up[0], preferred_element_type=jnp.float32)
    hidden = (jax.nn.silu(gate_out) * up_out).astype(jnp.bfloat16)
    down_piece = jnp.dot(hidden, w_down[0], preferred_element_type=jnp.float32).astype(jnp.bfloat16)
    returned = lax.all_to_all(
        down_piece.reshape(arrived.shape), "expert", split_axis=0, concat_axis=0, tiled=True
    )
    picked = returned.reshape(-1, model_width)[slot_flat]
    mix_share = weight_first[:, None] * picked[:, 0].astype(jnp.float32) + weight_second[
        :, None
    ] * picked[:, 1].astype(jnp.float32)
    mixture = lax.psum(mix_share, "ffn")
    layer_out = (token_rows.astype(jnp.float32) + mixture).astype(jnp.bfloat16)
    own_cols = lax.dynamic_slice_in_dim(layer_out, column, col_count, 1)
    adapted = (
        own_cols.astype(jnp.float32)
        + jnp.dot(layer_out, adapter[0], preferred_element_type=jnp.float32)
    ).astype(jnp.bfloat16)
    grad_input = upstream[0]
    adapter_grad = lax.dot_general(
        layer_out, grad_input, (((0,), (0,)), ((), ())), preferred_element_type=jnp.float32
    )
    cotangent_gram = lax.dot_general(
        grad_input, grad_input, (((1,), (1,)), ((), ())), preferred_element_type=jnp.float32
    )
    whole_gram = lax.psum(cotangent_gram, "ffn")
    layer_gram = lax.dot_general(
        layer_out, layer_out, (((1,), (1,)), ((), ())), preferred_element_type=jnp.float32
    )
    squared = jnp.sum(layer_gram * whole_gram)
    grad_norm = jnp.sqrt(squared)
    clip_limit = bound[0]
    factor = clip_limit / jnp.maximum(grad_norm, clip_limit)
    clipped = (adapter_grad * factor).astype(jnp.bfloat16)
    return (adapted[None], clipped[None])


def solution(mesh):
    in_specs = (
        P("expert", "ffn", None),
        P("expert", None, None),
        P(),
        P("expert", None, "ffn"),
        P("expert", None, "ffn"),
        P("expert", "ffn", None),
        P("expert", None, "ffn"),
        P("expert", None, "ffn"),
        P("expert"),
    )
    out_specs = (P("expert", None, "ffn"), P("expert", None, "ffn"))
    return jax.shard_map(
        per_device, mesh=mesh, in_specs=in_specs, out_specs=out_specs, check_vma=False
    )
```

profile of v0, /device:TPU:0, one launch (start us, length us, event | category | flops | bytes accessed | tf_op | source)
XLA Modules:
  0.0 190.7 jit_solution(15884546444229429780)
XLA Ops:
  7.2 0.0 copy-start
  7.2 0.0 copy-start.1
  7.2 0.7 shift-left_or_fusion
  7.9 0.8 copy.46
  8.6 0.7 convert_reduce_fusion
  9.3 0.1 copy.47
  9.4 0.1 copy.44
  9.5 0.1 reshape.206
  9.6 0.1 reduce_window_sum.11
  9.7 0.1 squeeze.35
  9.8 0.1 reshape.222
  9.9 0.0 copy-start.3
  9.9 0.8 gather_fusion.3
  10.7 0.8 scatter_custom_fusion
  11.5 0.0 copy-done.1
  11.6 0.1 copy.43
  11.6 33.0 %all_gather.3 = bf16[1,32,4096]{2,0,1:T(2,128)(2,1)S(1)} all-gather(bf16[1,4,4096]{2,0,1:T(2,128)(2,1)S(1)} %copy.43), channel_id=1, replica_groups=mesh['expert'=4,'ffn'=8] {'ffn'}, dimensions={1}, use_global_device_ids=true | all-gather | bytes 294912 | tf_op jit(solution)/shard_map/all_gather | solution.py:42
  44.6 0.3 copy.65
  45.0 1.9 %gather_fusion = bf16[96,4096]{1,0:T(8,128)(2,1)} fusion(bf16[33,4096]{1,0:T(8,128)(2,1)S(1)} %concatenate.3, s32[1024]{0:T(1024)S(1)} %pad_clamp_fusion.1), kind=kCustom, calls=%fused_computation | custom fusion | bytes 1573248 | tf_op jit(solution)/shard_map/gather | solution.py:30
  46.9 3.5 %all-to-all-start = ((bf16[4,24,4096]{2,1,0:T(8,128)(2,1)}), bf16[4,24,4096]{2,1,0:T(8,128)(2,1)S(1)}, u32[]{:S(2)}, u32[]{:S(2)}) async-start(bf16[4,24,4096]{2,1,0:T(8,128)(2,1)} %bitcast.5), calls=%async_computation | async-start | bytes 1572864 | tf_op jit(solution)/shard_map/all_to_all | solution.py:52
  50.4 0.1 gather.22
  50.5 0.1 copy.49
  50.6 0.2 fusion.43
  50.8 11.2 %all-to-all-done = bf16[4,24,4096]{2,1,0:T(8,128)(2,1)S(1)} async-done(((bf16[4,24,4096]{2,1,0:T(8,128)(2,1)}), bf16[4,24,4096]{2,1,0:T(8,128)(2,1)S(1)}, u32[]{:S(2)}, u32[]{:S(2)}) %all-to-all-start) | async-done | bytes 786464 | tf_op jit(solution)/shard_map/all_to_all | solution.py:52
  62.0 6.7 %fusion.4 = f32[96,1536]{1,0:T(8,128)S(1)} fusion(bf16[96,4096]{1,0:T(8,128)(2,1)S(1)} %bitcast.93, bf16[1,4096,1536]{2,1,0:T(8,128)(2,1)} %param.12), kind=kOutput, calls=%fused_computation.9 | convolution fusion | flops 1207959552 | bytes 13959168 | tf_op jit(solution)/shard_map/dot_general | solution.py:54
  68.6 0.0 copy-start.2
  68.7 13.3 %fusion.7 = bf16[96,4096]{1,0:T(8,128)(2,1)} fusion(bf16[1,1536,4096]{2,1,0:T(8,128)(2,1)} %param.14, bf16[96,4096]{1,0:T(8,128)(2,1)S(1)} %bitcast.94, bf16[1,4096,1536]{2,1,0:T(8,128)(2,1)} %param.13, f32[96,1536]{1,0:T(8,128)S(1)} %fusion.4), kind=kOutput, calls=%fused_computation.13 | convolution fusion | flops 2417197056 | bytes 27328512 | tf_op jit(solution)/shard_map/dot_general | solution.py:57
  82.0 3.5 %all-to-all-start.1 = ((bf16[4,24,4096]{2,1,0:T(8,128)(2,1)}), bf16[4,24,4096]{2,1,0:T(8,128)(2,1)S(1)}, u32[]{:S(2)}, u32[]{:S(2)}) async-start(bf16[4,24,4096]{2,1,0:T(8,128)(2,1)} %bitcast.10), calls=%async_computation.1 | async-start | bytes 1572864 | tf_op jit(solution)/shard_map/all_to_all | solution.py:58
  85.5 0.0 all-reduce.3.cloned.1.call-start
  85.5 0.1 copy.50
  85.6 0.1 reshape.200
  85.7 0.9 gather_fusion.2
  86.6 0.1 reshape.209
  86.7 0.1 copy.45
  86.8 10.2 %all-to-all-done.1 = bf16[4,24,4096]{2,1,0:T(8,128)(2,1)S(1)} async-done(((bf16[4,24,4096]{2,1,0:T(8,128)(2,1)}), bf16[4,24,4096]{2,1,0:T(8,128)(2,1)S(1)}, u32[]{:S(2)}, u32[]{:S(2)}) %all-to-all-start.1) | async-done | bytes 786464 | tf_op jit(solution)/shard_map/all_to_all | solution.py:58
  97.0 0.9 gather_fusion.1
  97.9 0.3 reshape.199
  98.3 1.2 fusion.42
  99.4 1.4 fusion.31
  100.9 0.0 all-reduce.3.cloned.1.call-update
  101.6 0.0 copy-done
  101.6 0.1 fusion.33
  101.7 37.4 %psum.15 = f32[32,32]{1,0:T(8,128)S(1)} all-reduce(f32[32,32]{1,0:T(8,128)S(1)} %fusion.33), channel_id=1, replica_groups=mesh['expert'=4,'ffn'=8] {'ffn'}, use_global_device_ids=true, to_apply=%region_4.5 | all-reduce | flops 1024 | bytes 8192 | tf_op jit(solution)/shard_map/psum | solution.py:79
  139.1 35.0 %all-reduce.3.cloned.1.call-done = f32[32,4096]{1,0:T(8,128)} async-done(((f32[32,4096]{1,0:T(8,128)}), f32[32,4096]{1,0:T(8,128)}) %all-reduce.3.cloned.1.call-update) | async-done | bytes 524304 | tf_op jit(solution)/shard_map/psum | solution.py:65
  174.1 1.4 add_convert_fusion
  175.4 0.8 fusion.30
  177.0 3.3 %fusion.6 = bf16[1,4096,512]{2,1,0:T(8,128)(2,1)} fusion(bf16[32,4096]{1,0:T(8,128)(2,1)S(1)} %add_convert_fusion, f32[]{:T(128)S(6)} %div.14, bf16[1,32,512]{2,1,0:T(8,128)(2,1)S(1)} %copy-done), kind=kOutput, calls=%fused_computation.12 | convolution fusion | flops 138412032 | bytes 4489220 | tf_op jit(solution)/shard_map/dot_general | solution.py:73
  180.2 3.6 %fusion.24 = bf16[1,32,512]{2,1,0:T(8,128)(2,1)} fusion(bf16[32,4096]{1,0:T(8,128)(2,1)S(1)} %add_convert_fusion, bf16[1,4096,512]{2,1,0:T(8,128)(2,1)} %param.15, s32[]{:T(128)S(6)} %select_n.91), kind=kOutput, calls=%fused_computation.20 | convolution fusion | flops 134266880 | bytes 4521988 | tf_op jit(solution)/shard_map/dot_general | solution.py:70
  (12 shorter events, 0.1 us)
Async XLA Ops:
  7.2 94.4 %copy-start = (bf16[1,32,512]{2,1,0:T(8,128)(2,1)S(1)}, bf16[1,32,512]{2,1,0:T(8,128)(2,1)}, u32[]{:S(2)}) copy-start(bf16[1,32,512]{2,1,0:T(8,128)(2,1)} %param.16) | copy-start | bytes 98308
  7.2 4.4 %copy-start.1 = (bf16[1,4,4096]{2,1,0:T(4,128)(2,1)S(1)}, bf16[1,4,4096]{2,1,0:T(4,128)(2,1)}, u32[]{:S(2)}) copy-start(bf16[1,4,4096]{2,1,0:T(4,128)(2,1)} %param.9) | copy-start | bytes 98308
  9.9 40.7 %copy-start.3 = (bf16[4096,4]{0,1:T(4,128)(2,1)S(1)}, bf16[4096,4]{0,1:T(4,128)(2,1)}, u32[]{:S(2)}) copy-start(bf16[4096,4]{0,1:T(4,128)(2,1)} %param.11) | copy-start | bytes 98308
  46.9 15.1 %all-to-all-start = ((bf16[4,24,4096]{2,1,0:T(8,128)(2,1)}), bf16[4,24,4096]{2,1,0:T(8,128)(2,1)S(1)}, u32[]{:S(2)}, u32[]{:S(2)}) async-start(bf16[4,24,4096]{2,1,0:T(8,128)(2,1)} %bitcast.5), calls=%async_computation | async-start | bytes 1572864 | tf_op jit(solution)/shard_map/all_to_all | solution.py:52
  68.6 16.9 %copy-start.2 = (s32[1,32,2]{1,2,0:T(2,128)S(1)}, s32[1,32,2]{1,2,0:T(2,128)}, u32[]{:S(2)}) copy-start(s32[1,32,2]{1,2,0:T(2,128)} %param.10) | copy-start | bytes 772
  82.0 15.1 %all-to-all-start.1 = ((bf16[4,24,4096]{2,1,0:T(8,128)(2,1)}), bf16[4,24,4096]{2,1,0:T(8,128)(2,1)S(1)}, u32[]{:S(2)}, u32[]{:S(2)}) async-start(bf16[4,24,4096]{2,1,0:T(8,128)(2,1)} %bitcast.10), calls=%async_computation.1 | async-start | bytes 1572864 | tf_op jit(solution)/shard_map/all_to_all | solution.py:58
  85.5 88.6 %all-reduce.3.cloned.1.call-start = ((), (), s32[]{:S(2)}) async-start(), calls=%async_computation.2 | async-start | bytes 1048576 | tf_op jit(solution)/shard_map/psum | solution.py:65
Sparse Core Ops, SparseCore 0:
  101.0 72.9 all-reduce.2
where the time goes:
time: 191 us
  blocking collectives  70.4 us (37%)
  waiting for transfers between devices  56.4 us (30%)
  matrix products  28 us (15%)
  between operations  15.6 us (8%)
  local copies, waits for them, and re-layouts  8.92 us (5%)
  starting transfers between devices  7.03 us (4%)
  other arithmetic  4.31 us (2%)
    psum x1, blocking collectives, per_device(): whole_gram = lax.psum(cotangent_gram, 'ffn')  37.4 us
    psum x1, waiting for transfers between devices, per_device(): mixture = lax.psum(mix_share, 'ffn')  35 us
    all_gather x1, blocking collectives, per_device(): gathered = lax.all_gather(tokens, 'ffn', axis=1, tiled=True)  33 us
    dot_general x1, matrix products, per_device(): jnp.dot(hidden, w_down[0], preferred_element_type=jnp.float32)  13.3 us
    all_to_all x1, waiting for transfers between devices, per_device(): lax.all_to_all(outgoing, 'expert', split_axis=0, concat_axis=0, tiled=True)  11.2 us
    all_to_all x1, waiting for transfers between devices, per_device(): lax.all_to_all(down_piece.reshape(arrived.shape), 'expert', split_axis=0,...  10.2 us
    dot_general x1, matrix products, per_device(): gate_out = jnp.dot(flat_rows, w_gate[0], preferred_element_type=jnp.float32)  6.66 us
  transfers between devices with their start and end apart: 3, of which 3 were waited for; matrix products, arithmetic and copies ran while one was open for 1% of the time, Pallas kernels for 0%

commit v1 on v0

--- a/solution.py
+++ b/solution.py
@@ -39,7 +39,7 @@
 
 def per_device(tokens, routes, router, w_gate, w_up, w_down, adapter, upstream, bound):
     expert_count = lax.axis_size("expert")
-    gathered = lax.all_gather(tokens, "ffn", axis=1, tiled=True)
+    gathered = jnp.concatenate(lax.all_gather(tokens, "ffn"), axis=1)
     token_rows = gathered[0]
     token_count = token_rows.shape[0]
     model_width = token_rows.shape[1]

time: 191 us -> 190 us (level)
  no operation moved by 1% of the time
where the time goes in v1:
time: 190 us
  blocking collectives  69.8 us (37%)
  waiting for transfers between devices  56.5 us (30%)
  matrix products  28 us (15%)
  between operations  15.6 us (8%)
  local copies, waits for them, and re-layouts  8.63 us (5%)
  starting transfers between devices  7.03 us (4%)
  other arithmetic  4.06 us (2%)
    psum x1, blocking collectives, per_device(): whole_gram = lax.psum(cotangent_gram, 'ffn')  37.3 us
    psum x1, waiting for transfers between devices, per_device(): mixture = lax.psum(mix_share, 'ffn')  35 us
    all_gather x1, blocking collectives, per_device(): gathered = jnp.concatenate(lax.all_gather(tokens, 'ffn'), axis=1)  32.6 us
    dot_general x1, matrix products, per_device(): jnp.dot(hidden, w_down[0], preferred_element_type=jnp.float32)  13.3 us
    all_to_all x1, waiting for transfers between devices, per_device(): lax.all_to_all(outgoing, 'expert', split_axis=0, concat_axis=0, tiled=True)  11.2 us
    all_to_all x1, waiting for transfers between devices, per_device(): lax.all_to_all(down_piece.reshape(arrived.shape), 'expert', split_axis=0,...  10.2 us
    dot_general x1, matrix products, per_device(): gate_out = jnp.dot(flat_rows, w_gate[0], preferred_element_type=jnp.float32)  6.66 us
  transfers between devices with their start and end apart: 3, of which 3 were waited for; matrix products, arithmetic and copies ran while one was open for 1% of the time, Pallas kernels for 0%

profile of v1, /device:TPU:0, one launch (start us, length us, event | category | flops | bytes accessed | tf_op | source)
XLA Modules:
  0.0 189.6 jit_solution(5550533679147058522)
XLA Ops:
  7.2 0.0 copy-start
  7.2 0.0 copy-start.1
  7.2 0.7 shift-left_or_fusion
  7.9 0.8 copy.35
  8.6 0.7 convert_reduce_fusion
  9.3 0.1 copy.36
  9.4 0.1 copy.33
  9.5 0.1 reshape.206
  9.6 0.1 reduce_window_sum.11
  9.7 0.1 squeeze.31
  9.8 0.1 reshape.222
  9.9 0.0 copy-start.3
  9.9 0.8 gather_fusion.3
  10.7 0.8 scatter_custom_fusion
  11.5 0.0 copy-done.1
  11.6 32.6 %all-gather = bf16[8,4,4096]{2,1,0:T(4,128)(2,1)S(1)} all-gather(bf16[1,4,4096]{2,1,0:T(4,128)(2,1)S(1)} %copy-done.1), channel_id=2, replica_groups=mesh['expert'=4,'ffn'=8] {'ffn'}, dimensions={0}, use_global_device_ids=true | all-gather | bytes 294912 | tf_op jit(solution)/shard_map/all_gather | solution.py:42
  44.1 0.1 squeeze_reshape.3
  44.2 1.9 %gather_fusion = bf16[96,4096]{1,0:T(8,128)(2,1)} fusion(bf16[33,4096]{1,0:T(8,128)(2,1)S(1)} %concatenate.3, s32[1024]{0:T(1024)S(1)} %pad_clamp_fusion.1), kind=kCustom, calls=%fused_computation | custom fusion | bytes 1573248 | tf_op jit(solution)/shard_map/gather | solution.py:30
  46.1 3.5 %all-to-all-start = ((bf16[4,24,4096]{2,1,0:T(8,128)(2,1)}), bf16[4,24,4096]{2,1,0:T(8,128)(2,1)S(1)}, u32[]{:S(2)}, u32[]{:S(2)}) async-start(bf16[4,24,4096]{2,1,0:T(8,128)(2,1)} %bitcast.5), calls=%async_computation | async-start | bytes 1572864 | tf_op jit(solution)/shard_map/all_to_all | solution.py:52
  49.6 0.1 gather.22
  49.7 0.1 copy.38
  49.8 0.0 copy-done.3
  49.8 0.2 fusion.43
  50.0 11.2 %all-to-all-done = bf16[4,24,4096]{2,1,0:T(8,128)(2,1)S(1)} async-done(((bf16[4,24,4096]{2,1,0:T(8,128)(2,1)}), bf16[4,24,4096]{2,1,0:T(8,128)(2,1)S(1)}, u32[]{:S(2)}, u32[]{:S(2)}) %all-to-all-start) | async-done | bytes 786464 | tf_op jit(solution)/shard_map/all_to_all | solution.py:52
  61.2 6.7 %fusion.4 = f32[96,1536]{1,0:T(8,128)S(1)} fusion(bf16[96,4096]{1,0:T(8,128)(2,1)S(1)} %bitcast.88, bf16[1,4096,1536]{2,1,0:T(8,128)(2,1)} %param.12), kind=kOutput, calls=%fused_computation.9 | convolution fusion | flops 1207959552 | bytes 13959168 | tf_op jit(solution)/shard_map/dot_general | solution.py:54
  67.9 0.0 copy-start.2
  67.9 13.3 %fusion.7 = bf16[96,4096]{1,0:T(8,128)(2,1)} fusion(bf16[1,1536,4096]{2,1,0:T(8,128)(2,1)} %param.14, bf16[96,4096]{1,0:T(8,128)(2,1)S(1)} %bitcast.89, bf16[1,4096,1536]{2,1,0:T(8,128)(2,1)} %param.13, f32[96,1536]{1,0:T(8,128)S(1)} %fusion.4), kind=kOutput, calls=%fused_computation.13 | convolution fusion | flops 2417197056 | bytes 27328512 | tf_op jit(solution)/shard_map/dot_general | solution.py:57
  81.2 3.5 %all-to-all-start.1 = ((bf16[4,24,4096]{2,1,0:T(8,128)(2,1)}), bf16[4,24,4096]{2,1,0:T(8,128)(2,1)S(1)}, u32[]{:S(2)}, u32[]{:S(2)}) async-start(bf16[4,24,4096]{2,1,0:T(8,128)(2,1)} %bitcast.10), calls=%async_computation.1 | async-start | bytes 1572864 | tf_op jit(solution)/shard_map/all_to_all | solution.py:58
  84.7 0.0 all-reduce.3.cloned.1.call-start
  84.7 0.0 copy-done.2
  84.8 0.1 copy.39
  84.9 0.1 reshape.200
  85.0 0.9 gather_fusion.2
  85.8 0.1 reshape.209
  86.0 0.1 copy.34
  86.1 10.2 %all-to-all-done.1 = bf16[4,24,4096]{2,1,0:T(8,128)(2,1)S(1)} async-done(((bf16[4,24,4096]{2,1,0:T(8,128)(2,1)}), bf16[4,24,4096]{2,1,0:T(8,128)(2,1)S(1)}, u32[]{:S(2)}, u32[]{:S(2)}) %all-to-all-start.1) | async-done | bytes 786464 | tf_op jit(solution)/shard_map/all_to_all | solution.py:58
  96.3 0.9 gather_fusion.1
  97.2 0.3 reshape.199
  97.5 1.2 fusion.42
  98.7 1.4 fusion.31
  100.1 0.0 all-reduce.3.cloned.1.call-update
  100.8 0.1 fusion.33
  100.9 37.3 %psum.15 = f32[32,32]{1,0:T(8,128)S(1)} all-reduce(f32[32,32]{1,0:T(8,128)S(1)} %fusion.33), channel_id=1, replica_groups=mesh['expert'=4,'ffn'=8] {'ffn'}, use_global_device_ids=true, to_apply=%region_4.5 | all-reduce | flops 1024 | bytes 8192 | tf_op jit(solution)/shard_map/psum | solution.py:79
  138.2 35.0 %all-reduce.3.cloned.1.call-done = f32[32,4096]{1,0:T(8,128)} async-done(((f32[32,4096]{1,0:T(8,128)}), f32[32,4096]{1,0:T(8,128)}) %all-reduce.3.cloned.1.call-update) | async-done | bytes 524304 | tf_op jit(solution)/shard_map/psum | solution.py:65
  173.2 1.1 add_convert_fusion
  174.3 0.8 fusion.30
  175.8 3.3 %fusion.6 = bf16[1,4096,512]{2,1,0:T(8,128)(2,1)} fusion(bf16[32,4096]{1,0:T(8,128)(2,1)S(1)} %add_convert_fusion, f32[]{:T(128)S(6)} %div.14, bf16[1,32,512]{2,1,0:T(8,128)(2,1)S(1)} %copy-done), kind=kOutput, calls=%fused_computation.12 | convolution fusion | flops 138412032 | bytes 4489220 | tf_op jit(solution)/shard_map/dot_general | solution.py:73
  179.1 3.6 %fusion.24 = bf16[1,32,512]{2,1,0:T(8,128)(2,1)} fusion(bf16[32,4096]{1,0:T(8,128)(2,1)S(1)} %add_convert_fusion, bf16[1,4096,512]{2,1,0:T(8,128)(2,1)} %param.15, s32[]{:T(128)S(6)} %select_n.91), kind=kOutput, calls=%fused_computation.20 | convolution fusion | flops 134266880 | bytes 4521988 | tf_op jit(solution)/shard_map/dot_general | solution.py:70
  (11 shorter events, 0.1 us)
Async XLA Ops:
  7.2 93.6 %copy-start = (bf16[1,32,512]{2,1,0:T(8,128)(2,1)S(1)}, bf16[1,32,512]{2,1,0:T(8,128)(2,1)}, u32[]{:S(2)}) copy-start(bf16[1,32,512]{2,1,0:T(8,128)(2,1)} %param.16) | copy-start | bytes 98308
  7.2 4.4 %copy-start.1 = (bf16[1,4,4096]{2,1,0:T(4,128)(2,1)S(1)}, bf16[1,4,4096]{2,1,0:T(4,128)(2,1)}, u32[]{:S(2)}) copy-start(bf16[1,4,4096]{2,1,0:T(4,128)(2,1)} %param.9) | copy-start | bytes 98308
  9.9 39.9 %copy-start.3 = (bf16[4096,4]{0,1:T(4,128)(2,1)S(1)}, bf16[4096,4]{0,1:T(4,128)(2,1)}, u32[]{:S(2)}) copy-start(bf16[4096,4]{0,1:T(4,128)(2,1)} %param.11) | copy-start | bytes 98308
  46.1 15.1 %all-to-all-start = ((bf16[4,24,4096]{2,1,0:T(8,128)(2,1)}), bf16[4,24,4096]{2,1,0:T(8,128)(2,1)S(1)}, u32[]{:S(2)}, u32[]{:S(2)}) async-start(bf16[4,24,4096]{2,1,0:T(8,128)(2,1)} %bitcast.5), calls=%async_computation | async-start | bytes 1572864 | tf_op jit(solution)/shard_map/all_to_all | solution.py:52
  67.9 16.9 %copy-start.2 = (s32[1,32,2]{1,2,0:T(2,128)S(1)}, s32[1,32,2]{1,2,0:T(2,128)}, u32[]{:S(2)}) copy-start(s32[1,32,2]{1,2,0:T(2,128)} %param.10) | copy-start | bytes 772
  81.2 15.1 %all-to-all-start.1 = ((bf16[4,24,4096]{2,1,0:T(8,128)(2,1)}), bf16[4,24,4096]{2,1,0:T(8,128)(2,1)S(1)}, u32[]{:S(2)}, u32[]{:S(2)}) async-start(bf16[4,24,4096]{2,1,0:T(8,128)(2,1)} %bitcast.10), calls=%async_computation.1 | async-start | bytes 1572864 | tf_op jit(solution)/shard_map/all_to_all | solution.py:58
  84.7 88.5 %all-reduce.3.cloned.1.call-start = ((), (), s32[]{:S(2)}) async-start(), calls=%async_computation.2 | async-start | bytes 1048576 | tf_op jit(solution)/shard_map/psum | solution.py:65
Sparse Core Ops, SparseCore 0:
  100.3 72.8 all-reduce.2
